TPU v7x, 512 devices: a whole 4x4x16 slice. The times are simulated.
512 devices in a mesh: grp: 16 (over z), cand: 32 (over y, x, core).
Axes of the slice: x: 4, y: 4, z: 16, core: 2. Of those that a mesh axis runs over, the one named last changes fastest.
Arguments:
- embeddings: bfloat16 [384, 1024, 1024], P('grp', 'cand'), may hold values from -6 to 6
- hidden_weight: bfloat16 [2048, 1024], P('cand'), may hold values from -0.1875 to 0.1875
- score_weight: bfloat16 [2048], replicated, may hold values from -0.5 to 0.5
- relevance: int32 [384, 1024], P('grp', 'cand'), may hold values from 0 to 4
- rank_pos: int32 [384, 1024], P('grp', 'cand'), may hold values from 0 to 1023, as said below
- ideal_dcg: float32 [384], P('grp'), may hold values from 32 to 128
Outputs:
- grad_hidden: float32 [2048, 1024], P('cand')
- lambdas: float32 [384, 1024], P('grp', 'cand')
Inputs may be any that keep to these rules, and one draw needn't show every extreme that they name: `rank_pos`: in each group the rank positions are a permutation of 0 to 1023.
All inputs are finite; a program needn't handle non-finite values.
Results may differ from a plain program's by a relative error of at most 0.006.
Values may be sent and summed in bfloat16 or wider, within the bound.
No kernel may reach another device: no remote copies, remote signals or barrier semaphores. Data moves between devices by JAX's collectives and lax.ppermute only.
A program may use at most 64 MiB of HBM per device.

v0:
```python
import jax
import jax.numpy as jnp
from jax import lax
from jax.sharding import PartitionSpec as P

EPS = 1e-06


def turned_gather(arrays, axis, dims):
    turned = [jnp.moveaxis(a, dim, 0) for a, dim in zip(arrays, dims)]
    widths = [t[0].size for t in turned]
    both = jnp.concatenate([t.reshape(-1, w) for t, w in zip(turned, widths)], axis=1)
    result = lax.all_gather(both, axis, axis=0, tiled=True)
    parts = jnp.split(result, [sum(widths[:k]) for k in range(1, len(widths))], axis=1)
    return tuple(
        (
            jnp.moveaxis(b.reshape(-1, *t.shape[1:]), 0, dim)
            for b, t, dim in zip(parts, turned, dims)
        )
    )


def copy_for_each(value, axis):
    copies = jnp.broadcast_to(value, (lax.axis_size(axis), *value.shape))
    return lax.all_to_all(copies, axis, split_axis=0, concat_axis=0, tiled=True)


def joined_along(parts, dim):
    parts = jnp.moveaxis(parts, 0, dim)
    shape = parts.shape
    return parts.reshape(*shape[:dim], shape[dim] * shape[dim + 1], *shape[dim + 2 :])


def gathered_copies(value, axis, dim):
    parts = copy_for_each(value, axis)
    return joined_along(parts, dim)


def over_copies(value, axis):
    return copy_for_each(value, axis).sum(axis=0)


def pair_lambdas(own_score, own_gain, own_disc, far_score, far_gain, far_disc, ideal):
    gain_diff = far_gain[..., None, :] - own_gain[..., :, None]
    toward = jnp.sign(gain_diff)
    weight = (
        jnp.abs(gain_diff)
        * jnp.abs(far_disc[..., None, :] - own_disc[..., :, None])
        / ideal[..., None, None]
    )
    margin = own_score[..., :, None] - far_score[..., None, :]
    return jnp.sum(weight * toward * jax.nn.sigmoid(toward * margin), axis=-1)


def gain_of(labels):
    return jnp.exp2(labels.astype(jnp.float32)) - 1.0


def discount_of(positions):
    return 1.0 / jnp.log2(2.0 + positions.astype(jnp.float32))


def per_device(embeddings, hidden_weight, score_weight, relevance, rank_pos, ideal_dcg):
    grp_count, local, width = embeddings.shape
    cand_rows = embeddings.reshape(grp_count * local, width)
    all_labels, all_ranks = turned_gather((relevance, rank_pos), "cand", (1, 1))
    all_gain = gain_of(all_labels)
    all_disc = discount_of(all_ranks)
    pre_act = lax.dot_general(
        cand_rows,
        lax.all_gather(hidden_weight, "cand", axis=0, tiled=True),
        (((1,), (1,)), ((), ())),
        preferred_element_type=jnp.float32,
    )
    acts, pull = jax.vjp(jax.nn.gelu, pre_act)
    scores = jnp.dot(
        acts.astype(jnp.bfloat16), score_weight, preferred_element_type=jnp.float32
    ).reshape(grp_count, local)
    gain_vals = gain_of(relevance)
    discount = discount_of(rank_pos)
    lambdas = pair_lambdas(
        scores,
        gain_vals,
        discount,
        gathered_copies(scores, "cand", 1),
        all_gain,
        all_disc,
        ideal_dcg,
    )
    upstream = (
        lambdas.reshape(grp_count * local)[:, None] * score_weight.astype(jnp.float32)[None, :]
    )
    grad_pre = pull(upstream)[0].astype(jnp.bfloat16)
    owned = lax.psum_scatter(
        lax.dot_general(
            grad_pre, cand_rows, (((0,), (0,)), ((), ())), preferred_element_type=jnp.float32
        ).astype(jnp.bfloat16),
        "cand",
        scatter_dimension=0,
        tiled=True,
    ).astype(jnp.float32)
    summed = lax.psum(owned, "grp")
    squares = over_copies(jnp.sum(summed * summed), "cand")
    entries = summed.shape[0] * summed.shape[1] * lax.axis_size("cand")
    scale = lax.rsqrt(squares / entries + EPS)
    return (summed * scale, lambdas)


def solution(mesh):
    return jax.shard_map(
        per_device,
        mesh=mesh,
        in_specs=(
            P("grp", "cand", None),
            P("cand", None),
            P(),
            P("grp", "cand"),
            P("grp", "cand"),
            P("grp"),
        ),
        out_specs=(P("cand", None), P("grp", "cand")),
        check_vma=False,
    )
```

profile of v0, /device:TPU:1, one launch (start us, length us, event | category | flops | bytes accessed | tf_op | source)
XLA Modules:
  0.0 302.9 jit_solution(5547443069772350048)
XLA Ops:
  7.2 0.0 copy-start
  7.2 0.0 all-gather.2.cloned.1.call-start
  7.2 0.7 all-gather.2.cloned.1.call-update
  7.9 0.7 reshape.20
  8.6 0.8 copy.28
  9.4 0.8 copy.29
  10.2 0.1 pad_add_fusion
  10.2 28.5 %all_gather.6 = s32[1024,48]{1,0:T(8,128)S(1)} all-gather(s32[32,48]{1,0:T(8,128)S(1)} %pad_add_fusion), channel_id=1, replica_groups=mesh['grp'=16,'cand'=32] {'cand'}, dimensions={0}, use_global_device_ids=true | all-gather | bytes 202752 | tf_op jit(solution)/shard_map/all_gather | solution.py:13
  38.7 0.2 fusion.33
  38.9 0.2 copy.35
  39.1 0.2 copy.36
  39.3 0.1 divide_bitcast_fusion
  39.3 38.9 %all-gather.2.cloned.1.call-done = bf16[2048,1024]{1,0:T(8,128)(2,1)} async-done(((bf16[64,1024]{1,0:T(8,128)(2,1)}), bf16[2048,1024]{1,0:T(8,128)(2,1)}) %all-gather.2.cloned.1.call-update) | async-done | bytes 4194320 | tf_op jit(solution)/shard_map/all_gather | solution.py:71
  78.2 0.0 copy-done
  78.2 5.3 %fusion.34 = f32[768,2048]{1,0:T(8,128)S(1)} fusion(bf16[768,1024]{1,0:T(8,128)(2,1)S(1)} %bitcast.12, bf16[2048,1024]{1,0:T(8,128)(2,1)} %all-gather.2.cloned.1.call-done), kind=kOutput, calls=%fused_computation.48 | convolution fusion | flops 3221225472 | bytes 12058624 | tf_op jit(solution)/shard_map/dot_general | solution.py:69
  83.5 0.0 copy-start.6
  83.5 2.7 copy-done.6
  86.1 0.0 copy-start.1
  86.1 0.0 copy-start.2
  86.1 0.0 copy-start.3
  86.1 0.0 copy-start.5
  86.1 2.2 fusion.22
  88.4 0.1 sub.63
  88.5 0.8 reshape.24
  89.3 5.3 %all-to-all-start = ((f32[32,1,768]{2,1,0:T(1,128)}), f32[32,1,768]{2,1,0:T(1,128)S(1)}, u32[]{:S(2)}, u32[]{:S(2)}) async-start(f32[32,1,768]{2,1,0:T(1,128)} %reshape.24), calls=%async_computation | async-start | bytes 196608 | tf_op jit(solution)/shard_map/all_to_all | solution.py:25
  94.6 0.0 reduce-scatter.2.cloned.1.call-start
  94.7 0.0 copy-done.1
  94.7 0.0 copy-done.2
  94.7 0.0 copy-done.3
  94.7 7.3 %all-to-all-done = f32[32,1,768]{2,1,0:T(1,128)S(1)} async-done(((f32[32,1,768]{2,1,0:T(1,128)}), f32[32,1,768]{2,1,0:T(1,128)S(1)}, u32[]{:S(2)}, u32[]{:S(2)}) %all-to-all-start) | async-done | bytes 98336 | tf_op jit(solution)/shard_map/all_to_all | solution.py:25
  102.0 0.5 broadcast.84
  102.5 0.9 reduce.3
  103.4 0.1 reshape.25
  103.6 0.1 copy.32
  103.6 0.2 sub.65
  103.8 0.0 copy-done.5
  103.8 3.0 fusion.13
  106.8 0.1 mul.88
  106.9 10.4 %convolution_convert_fusion = bf16[2048,1024]{1,0:T(8,128)(2,1)} fusion(bf16[768,1024]{1,0:T(8,128)(2,1)S(1)} %bitcast.13, f32[768,2048]{1,0:T(8,128)} %copy-done.6, f32[2048]{0:T(1024)S(1)} %convert_element_type.34, f32[768]{0:T(1024)S(1)} %mul.88), kind=kOutput, calls=%fused_computation.19 | convolution fusion | flops 3256352768 | bytes 12069888 | tf_op jit(solution)/shard_map/dot_general | solution.py:95
  117.3 0.0 copy-done.4
  117.3 0.0 reduce-scatter.2.cloned.1.call-update
  117.3 101.5 %reduce-scatter.2.cloned.1.call-done = bf16[64,1024]{1,0:T(8,128)(2,1)} async-done(((bf16[2048,1024]{1,0:T(8,128)(2,1)}), bf16[64,1024]{1,0:T(8,128)(2,1)}) %reduce-scatter.2.cloned.1.call-update) | async-done | bytes 131088 | tf_op jit(solution)/shard_map/reduce_scatter | solution.py:94
  218.8 46.8 %all-reduce.1 = f32[64,1024]{1,0:T(8,128)S(1)} all-reduce(bf16[64,1024]{1,0:T(8,128)(2,1)} %reduce-scatter.2.cloned.1.call-done), channel_id=1, replica_groups=mesh['grp'=16,'cand'=32] {'grp'}, use_global_device_ids=true, to_apply=%region_2.0 | all-reduce | flops 65536 | bytes 393216 | tf_op jit(solution)/shard_map/psum | solution.py:102
  265.6 0.7 multiply_reduce_fusion
  266.2 0.7 broadcast_in_dim.5
  266.9 27.1 %all_to_all.11 = f32[32,1,1]{2,1,0:T(1,128)S(1)} all-to-all(f32[32,1,1]{2,1,0:T(1,128)S(1)} %broadcast_in_dim.5), channel_id=1, replica_groups=mesh['grp'=16,'cand'=32] {'cand'}, dimensions={0} | all-to-all | bytes 256 | tf_op jit(solution)/shard_map/all_to_all | solution.py:25
  294.0 0.6 reduce_sum.29
  295.4 0.7 broadcast_multiply_fusion
  (4 shorter events, 0.1 us)
Async XLA Ops:
  7.2 71.0 %copy-start = (bf16[24,32,1024]{2,1,0:T(8,128)(2,1)S(1)}, bf16[24,32,1024]{2,1,0:T(8,128)(2,1)}, u32[]{:S(2)}) copy-start(bf16[24,32,1024]{2,1,0:T(8,128)(2,1)} %param.6) | copy-start | bytes 4718596
  7.2 71.0 %all-gather.2.cloned.1.call-start = ((), (), s32[]{:S(2)}) async-start(), calls=%async_computation.3 | async-start | bytes 4325376 | tf_op jit(solution)/shard_map/all_gather | solution.py:71
  83.5 2.7 copy-start.6
  86.1 8.6 %copy-start.1 = (s32[24,32]{1,0:T(8,128)S(1)}, s32[24,32]{1,0:T(8,128)}, u32[]{:S(2)}) copy-start(s32[24,32]{1,0:T(8,128)} %param.10) | copy-start | bytes 9220
  86.1 8.6 %copy-start.2 = (s32[24,32]{1,0:T(8,128)S(1)}, s32[24,32]{1,0:T(8,128)}, u32[]{:S(2)}) copy-start(s32[24,32]{1,0:T(8,128)} %param.9) | copy-start | bytes 9220
  86.1 8.6 %copy-start.3 = (bf16[2048]{0:T(1024)(128)(2,1)S(1)}, bf16[2048]{0:T(1024)(128)(2,1)}, u32[]{:S(2)}) copy-start(bf16[2048]{0:T(1024)(128)(2,1)} %param.8) | copy-start | bytes 12292
  86.1 17.7 %copy-start.5 = (f32[24]{0:T(128)S(1)}, f32[24]{0:T(128)}, u32[]{:S(2)}) copy-start(f32[24]{0:T(128)} %param.11) | copy-start | bytes 292
  89.3 12.7 %all-to-all-start = ((f32[32,1,768]{2,1,0:T(1,128)}), f32[32,1,768]{2,1,0:T(1,128)S(1)}, u32[]{:S(2)}, u32[]{:S(2)}) async-start(f32[32,1,768]{2,1,0:T(1,128)} %reshape.24), calls=%async_computation | async-start | bytes 196608 | tf_op jit(solution)/shard_map/all_to_all | solution.py:25
  94.6 124.2 %reduce-scatter.2.cloned.1.call-start = ((), (), s32[]{:S(2)}) async-start(), calls=%async_computation.4 | async-start | bytes 4325376 | tf_op jit(solution)/shard_map/reduce_scatter | solution.py:94
  106.8 10.5 %copy-start.4 = (f32[24,32]{1,0:T(8,128)}, f32[24,32]{1,0:T(8,128)S(1)}, u32[]{:S(2)}) copy-start(f32[24,32]{1,0:T(8,128)S(1)} %fusion.13) | copy-start | bytes 9220
Sparse Core Ops, SparseCore 0:
  11.1 67.0 all-gather.1
  117.5 101.2 reduce-scatter.1
where the time goes:
time: 303 us
  waiting for transfers between devices  148 us (49%)
  blocking collectives  102 us (34%)
  matrix products  17.9 us (6%)
  between operations  14.9 us (5%)
  local copies, waits for them, and re-layouts  8.06 us (3%)
  other arithmetic  6.06 us (2%)
  starting transfers between devices  5.38 us (2%)
    reduce_scatter x1, waiting for transfers between devices, per_device(): lax.psum_scatter(lax.dot_general(grad_pre, cand_rows, (((0,), (0,)), ((),...  101 us
    psum x1, blocking collectives, per_device(): summed = lax.psum(owned, 'grp')  46.8 us
    all_gather x1, waiting for transfers between devices, per_device(): lax.all_gather(hidden_weight, 'cand', axis=0, tiled=True)  38.9 us
    all_gather x1, blocking collectives, turned_gather(): result = lax.all_gather(both, axis, axis=0, tiled=True)  28.5 us
    all_to_all x1, blocking collectives, copy_for_each(): return lax.all_to_all(copies, axis, split_axis=0, concat_axis=0, tiled=True)  27.1 us
    dot_general x1, matrix products, per_device(): lax.dot_general(grad_pre, cand_rows, (((0,), (0,)), ((), ())), preferred_...  10.4 us
    all_to_all x1, waiting for transfers between devices, copy_for_each(): return lax.all_to_all(copies, axis, split_axis=0, concat_axis=0, tiled=True)  7.27 us
    unnamed x21, local copies, waits for them, and re-layouts  6.27 us
  transfers between devices with their start and end apart: 3, of which 3 were waited for; matrix products, arithmetic and copies ran while one was open for 1% of the time, Pallas kernels for 0%

commit v1 on v0

--- a/solution.py
+++ b/solution.py
@@ -10,7 +10,9 @@
     turned = [jnp.moveaxis(a, dim, 0) for a, dim in zip(arrays, dims)]
     widths = [t[0].size for t in turned]
     both = jnp.concatenate([t.reshape(-1, w) for t, w in zip(turned, widths)], axis=1)
-    result = lax.all_gather(both, axis, axis=0, tiled=True)
+    result = jnp.concatenate(
+        lax.all_to_all(jnp.stack([both] * lax.axis_size(axis)), axis, 0, 0), axis=0
+    )
     parts = jnp.split(result, [sum(widths[:k]) for k in range(1, len(widths))], axis=1)
     return tuple(
         (

time: 303 us -> 304 us (level)
  blocking collectives: 102 us -> 73.9 us
  waiting for transfers between devices: 148 us -> 163 us
  starting transfers between devices: 5.38 us -> 15.7 us
  other arithmetic: 6.06 us -> 9.23 us
    all_gather x1 -> x0, blocking collectives: 28.5 us -> none  [turned_gather(): result = lax.all_gather(both, axis, axis=0, tiled=True)]
    all_to_all x0 -> x1, starting transfers between devices: none -> 10.4 us  [turned_gather(): lax.all_to_all(jnp.stack([both] * lax.axis_size(axis)), axis, 0, 0)]
    all_gather x1, waiting for transfers between devices: 38.9 us -> 47.1 us  [per_device(): lax.all_gather(hidden_weight, 'cand', axis=0, tiled=True)]
    all_to_all x0 -> x1, waiting for transfers between devices: none -> 6.22 us  [turned_gather(): lax.all_to_all(jnp.stack([both] * lax.axis_size(axis)), axis, 0, 0)]
    unnamed x21 -> x15, local copies, waits for them, and re-layouts: 6.27 us -> 6.11 us
  transfers between devices with their start and end apart: 3 -> 4, of which waited for: 3 -> 4; matrix products, arithmetic and copies ran while one was open for 1% -> 2% of each run, Pallas kernels for 0% -> 0%
where the time goes in v1:
time: 304 us; the launch traced here: 303 us
  waiting for transfers between devices  163 us (54%)
  blocking collectives  73.9 us (24%)
  matrix products  17.9 us (6%)
  starting transfers between devices  15.7 us (5%)
  between operations  14.9 us (5%)
  other arithmetic  9.23 us (3%)
  local copies, waits for them, and re-layouts  8.55 us (3%)
    reduce_scatter x1, waiting for transfers between devices, per_device(): lax.psum_scatter(lax.dot_general(grad_pre, cand_rows, (((0,), (0,)), ((),...  102 us
    all_gather x1, waiting for transfers between devices, per_device(): lax.all_gather(hidden_weight, 'cand', axis=0, tiled=True)  47.1 us
    psum x1, blocking collectives, per_device(): summed = lax.psum(owned, 'grp')  46.6 us
    all_to_all x1, blocking collectives, copy_for_each(): return lax.all_to_all(copies, axis, split_axis=0, concat_axis=0, tiled=True)  27.3 us
    dot_general x1, matrix products, per_device(): lax.dot_general(grad_pre, cand_rows, (((0,), (0,)), ((), ())), preferred_...  10.4 us
    all_to_all x1, starting transfers between devices, turned_gather(): lax.all_to_all(jnp.stack([both] * lax.axis_size(axis)), axis, 0, 0)  10.4 us
    all_to_all x1, waiting for transfers between devices, copy_for_each(): return lax.all_to_all(copies, axis, split_axis=0, concat_axis=0, tiled=True)  7.28 us
    all_to_all x1, waiting for transfers between devices, turned_gather(): lax.all_to_all(jnp.stack([both] * lax.axis_size(axis)), axis, 0, 0)  6.22 us
  transfers between devices with their start and end apart: 4, of which 4 were waited for; matrix products, arithmetic and copies ran while one was open for 2% of the time, Pallas kernels for 0%

profile of v1, /device:TPU:1, one launch (start us, length us, event | category | flops | bytes accessed | tf_op | source)
XLA Modules:
  0.0 303.0 jit_solution(16911326191457132690)
XLA Ops:
  7.2 0.0 copy-start
  7.2 0.0 all-gather.2.cloned.1.call-start
  7.2 0.7 all-gather.2.cloned.1.call-update
  7.9 0.7 pad_add_fusion
  8.6 0.1 copy.20
  8.7 0.1 stack.2
  8.8 1.2 reshape.32
  10.0 10.4 %all-to-all-start = ((s32[32,1,1536]{2,1,0:T(1,128)}), s32[32,1,1536]{2,1,0:T(1,128)S(1)}, u32[]{:S(2)}, u32[]{:S(2)}) async-start(s32[32,1,1536]{2,1,0:T(1,128)} %reshape.32), calls=%async_computation | async-start | bytes 393216 | tf_op jit(solution)/shard_map/all_to_all | solution.py:14
  20.3 0.7 reshape.26
  21.0 0.7 convert_element_type.34
  21.7 0.7 multiply_divide_fusion
  22.5 6.2 %all-to-all-done = s32[32,1,1536]{2,1,0:T(1,128)S(1)} async-done(((s32[32,1,1536]{2,1,0:T(1,128)}), s32[32,1,1536]{2,1,0:T(1,128)S(1)}, u32[]{:S(2)}, u32[]{:S(2)}) %all-to-all-start) | async-done | bytes 196640 | tf_op jit(solution)/shard_map/all_to_all | solution.py:14
  28.7 0.5 broadcast.87
  29.2 1.1 reduce.4
  30.3 0.2 reshape.33
  30.6 0.2 fusion.33
  30.8 0.2 copy.26
  30.9 0.2 copy.27
  31.1 47.1 %all-gather.2.cloned.1.call-done = bf16[2048,1024]{1,0:T(8,128)(2,1)} async-done(((bf16[64,1024]{1,0:T(8,128)(2,1)}), bf16[2048,1024]{1,0:T(8,128)(2,1)}) %all-gather.2.cloned.1.call-update) | async-done | bytes 4194320 | tf_op jit(solution)/shard_map/all_gather | solution.py:73
  78.2 0.0 copy-done
  78.2 5.3 %fusion.34 = f32[768,2048]{1,0:T(8,128)S(1)} fusion(bf16[768,1024]{1,0:T(8,128)(2,1)S(1)} %bitcast.13, bf16[2048,1024]{1,0:T(8,128)(2,1)} %all-gather.2.cloned.1.call-done), kind=kOutput, calls=%fused_computation.48 | convolution fusion | flops 3221225472 | bytes 12058624 | tf_op jit(solution)/shard_map/dot_general | solution.py:71
  83.5 0.0 copy-start.3
  83.5 2.7 copy-done.3
  86.1 2.2 fusion.22
  88.3 0.1 sub.63
  88.4 0.8 reshape.30
  89.3 5.3 %all-to-all-start.1 = ((f32[32,1,768]{2,1,0:T(1,128)}), f32[32,1,768]{2,1,0:T(1,128)S(1)}, u32[]{:S(2)}, u32[]{:S(2)}) async-start(f32[32,1,768]{2,1,0:T(1,128)} %reshape.30), calls=%async_computation.1 | async-start | bytes 196608 | tf_op jit(solution)/shard_map/all_to_all | solution.py:27
  94.6 0.0 reduce-scatter.2.cloned.1.call-start
  94.6 0.1 divide_bitcast_fusion
  94.7 7.3 %all-to-all-done.1 = f32[32,1,768]{2,1,0:T(1,128)S(1)} async-done(((f32[32,1,768]{2,1,0:T(1,128)}), f32[32,1,768]{2,1,0:T(1,128)S(1)}, u32[]{:S(2)}, u32[]{:S(2)}) %all-to-all-start.1) | async-done | bytes 98336 | tf_op jit(solution)/shard_map/all_to_all | solution.py:27
  102.0 0.5 broadcast.86
  102.5 0.9 reduce.3
  103.4 0.1 reshape.31
  103.5 0.1 copy.22
  103.6 0.2 sub.65
  103.8 0.0 copy-done.2
  103.8 3.0 fusion.13
  106.8 0.1 mul.88
  106.9 10.4 %convolution_convert_fusion = bf16[2048,1024]{1,0:T(8,128)(2,1)} fusion(bf16[768,1024]{1,0:T(8,128)(2,1)S(1)} %bitcast.14, f32[768,2048]{1,0:T(8,128)} %copy-done.3, f32[2048]{0:T(1024)S(1)} %convert_element_type.34, f32[768]{0:T(1024)S(1)} %mul.88), kind=kOutput, calls=%fused_computation.19 | convolution fusion | flops 3256352768 | bytes 12069888 | tf_op jit(solution)/shard_map/dot_general | solution.py:97
  117.3 0.0 copy-done.1
  117.3 0.0 reduce-scatter.2.cloned.1.call-update
  117.3 101.5 %reduce-scatter.2.cloned.1.call-done = bf16[64,1024]{1,0:T(8,128)(2,1)} async-done(((bf16[2048,1024]{1,0:T(8,128)(2,1)}), bf16[64,1024]{1,0:T(8,128)(2,1)}) %reduce-scatter.2.cloned.1.call-update) | async-done | bytes 131088 | tf_op jit(solution)/shard_map/reduce_scatter | solution.py:96
  218.8 46.6 %all-reduce.1 = f32[64,1024]{1,0:T(8,128)S(1)} all-reduce(bf16[64,1024]{1,0:T(8,128)(2,1)} %reduce-scatter.2.cloned.1.call-done), channel_id=1, replica_groups=mesh['grp'=16,'cand'=32] {'grp'}, use_global_device_ids=true, to_apply=%region_2.0 | all-reduce | flops 65536 | bytes 393216 | tf_op jit(solution)/shard_map/psum | solution.py:104
  265.4 0.7 multiply_reduce_fusion
  266.1 0.7 broadcast_in_dim.5
  266.8 27.3 %all_to_all.16 = f32[32,1,1]{2,1,0:T(1,128)S(1)} all-to-all(f32[32,1,1]{2,1,0:T(1,128)S(1)} %broadcast_in_dim.5), channel_id=1, replica_groups=mesh['grp'=16,'cand'=32] {'cand'}, dimensions={0} | all-to-all | bytes 256 | tf_op jit(solution)/shard_map/all_to_all | solution.py:27
  294.1 0.6 reduce_sum.29
  295.4 0.7 broadcast_multiply_fusion
  (3 shorter events, 0.0 us)
Async XLA Ops:
  7.2 71.0 %copy-start = (bf16[24,32,1024]{2,1,0:T(8,128)(2,1)S(1)}, bf16[24,32,1024]{2,1,0:T(8,128)(2,1)}, u32[]{:S(2)}) copy-start(bf16[24,32,1024]{2,1,0:T(8,128)(2,1)} %param.6) | copy-start | bytes 4718596
  7.2 71.0 %all-gather.2.cloned.1.call-start = ((), (), s32[]{:S(2)}) async-start(), calls=%async_computation.4 | async-start | bytes 4325376 | tf_op jit(solution)/shard_map/all_gather | solution.py:73
  10.0 18.7 %all-to-all-start = ((s32[32,1,1536]{2,1,0:T(1,128)}), s32[32,1,1536]{2,1,0:T(1,128)S(1)}, u32[]{:S(2)}, u32[]{:S(2)}) async-start(s32[32,1,1536]{2,1,0:T(1,128)} %reshape.32), calls=%async_computation | async-start | bytes 393216 | tf_op jit(solution)/shard_map/all_to_all | solution.py:14
  83.5 2.7 copy-start.3
  86.1 17.7 %copy-start.2 = (f32[24]{0:T(128)S(1)}, f32[24]{0:T(128)}, u32[]{:S(2)}) copy-start(f32[24]{0:T(128)} %param.11) | copy-start | bytes 292
  89.3 12.7 %all-to-all-start.1 = ((f32[32,1,768]{2,1,0:T(1,128)}), f32[32,1,768]{2,1,0:T(1,128)S(1)}, u32[]{:S(2)}, u32[]{:S(2)}) async-start(f32[32,1,768]{2,1,0:T(1,128)} %reshape.30), calls=%async_computation.1 | async-start | bytes 196608 | tf_op jit(solution)/shard_map/all_to_all | solution.py:27
  94.6 124.2 %reduce-scatter.2.cloned.1.call-start = ((), (), s32[]{:S(2)}) async-start(), calls=%async_computation.5 | async-start | bytes 4325376 | tf_op jit(solution)/shard_map/reduce_scatter | solution.py:96
  106.8 10.5 %copy-start.1 = (f32[24,32]{1,0:T(8,128)}, f32[24,32]{1,0:T(8,128)S(1)}, u32[]{:S(2)}) copy-start(f32[24,32]{1,0:T(8,128)S(1)} %fusion.13) | copy-start | bytes 9220
Sparse Core Ops, SparseCore 0:
  11.1 67.0 all-gather.1
  117.4 101.3 reduce-scatter.1
